TPU v7x, 32 devices: a whole 2x2x4 slice. The times are simulated.
32 devices in a mesh: farcp: 2 (over x), nearcp: 4 (over y, core), model: 4 (over z).
Axes of the slice: x: 2, y: 2, z: 4, core: 2. Of those that a mesh axis runs over, the one named last changes fastest.
Arguments:
- raw_keys: bfloat16 [8, 8192, 8, 128], P(None, ('farcp', 'nearcp'), 'model'), may hold values from -6 to 6
- raw_values: bfloat16 [8, 8192, 8, 128], P(None, ('farcp', 'nearcp'), 'model'), may hold values from -6 to 6
- turn_angle: float32 [8192, 64], replicated, may hold values from -3.140625 to 3.140625
- key_gain: float32 [128], replicated, may hold values from 0.25 to 1.75
Outputs:
- stored_keys: bfloat16 [8, 8192, 8, 128], P(('farcp', 'nearcp'), None, 'model')
- stored_values: bfloat16 [8, 8192, 8, 128], P(('farcp', 'nearcp'), None, 'model')
- key_scale: float32 [8, 8, 128], P(('farcp', 'nearcp'), 'model')
All inputs are finite; a program needn't handle non-finite values. Where the computation divides by a largest or mean magnitude, that divisor is 1e-20 or more.
Results may differ from a plain program's by a relative error of at most 0.001.
Values may be sent and summed in bfloat16 or wider, within the bound.
A program may use at most 192 MiB of HBM per device.

v0:
```python
import functools

import jax
import jax.numpy as jnp
from jax import lax
from jax.experimental import pallas as pl
from jax.experimental.pallas import tpu as pltpu
from jax.sharding import PartitionSpec as P

FAR, NEAR = "farcp", "nearcp"
MESH_ID = pl.DeviceIdType.MESH
TILE = 256
PARTS = 1
WRITES = 4
LANES = 128


def moved_index(index, step, size, sign):
    if size & (size - 1):
        return (index + sign * step + size) % size
    bit = 1
    while bit < size:
        index = index + ((step // bit) % 2) * (bit - 2 * bit * ((index // bit) % 2))
        bit *= 2
    return index


def partner_orders(far_size, near_size):
    both, first, second, same = [], [], [], []
    for step in range(1, far_size * near_size):
        far, chip = step // near_size > 0, step % near_size > 1
        (both if far and chip else first if far else second if chip else same).append(step)
    orders = []
    for lists in ((both, first, second), (first, both, second)):
        order = []
        for turn in range(max(map(len, lists))):
            order += [steps[turn] for steps in lists if turn < len(steps)]
        orders.append(order + same)
    return orders


def exchange_kernel(
    far_size, near_size, heads, keys_ref, values_ref, turn_ref, plain_gain_ref,
    out_keys, out_values, out_scale,
    angle_ref, gain_ref, landed, cos_table, sin_table, turned, send_sem, recv_sem, local_sem,
):
    far, near = lax.axis_index(FAR), lax.axis_index(NEAR)
    me = far * near_size + near
    rows = keys_ref.shape[1]
    total_rows = landed.shape[0]
    half = angle_ref.shape[0]
    even, odd = partner_orders(far_size, near_size)
    part = rows // PARTS

    def device(step, sign):
        return (
            moved_index(far, step // near_size, far_size, sign),
            moved_index(near, step % near_size, near_size, sign),
        )

    barrier = pltpu.get_barrier_semaphore()
    for step in even:
        f, n = device(step, 1)
        pl.semaphore_signal(barrier, inc=1, device_id={FAR: f, NEAR: n}, device_id_type=MESH_ID)
    angles = pltpu.make_async_copy(turn_ref, angle_ref, local_sem.at[2])
    angles.start()
    gains = pltpu.make_async_copy(plain_gain_ref, gain_ref, local_sem.at[3])
    gains.start()
    own = [
        pltpu.make_async_copy(src.at[me], dst.at[pl.ds(me * rows, rows)], local_sem.at[i])
        for i, (src, dst) in enumerate(((keys_ref, landed), (values_ref, out_values)))
    ]
    for copy in own:
        copy.start()

    def remote(which, piece, step):
        src, dst = ((keys_ref, landed), (values_ref, out_values))[which]
        f, n = device(step, 1)
        return pltpu.make_async_remote_copy(
            src_ref=src.at[f * near_size + n, pl.ds(piece * part, part)],
            dst_ref=dst.at[pl.ds(me * rows + piece * part, part)],
            send_sem=send_sem.at[which, piece, step],
            recv_sem=recv_sem.at[which, piece, step],
            device_id={FAR: f, NEAR: n},
            device_id_type=MESH_ID,
        )

    pl.semaphore_wait(barrier, len(even))
    for which in range(2):
        for piece in range(PARTS):
            for a, b in zip(even, odd):
                remote(which, piece, a + (b - a) * (me % 2)).start()

    angles.wait()
    gains.wait()
    gain = gain_ref[...]
    other_gain = pltpu.roll(gain, half, 1)

    def fill(block, carry):
        angle = angle_ref[:, pl.ds(pl.multiple_of(block * LANES, LANES), LANES)]
        cosine, sine = jnp.cos(angle), jnp.sin(angle)
        cosine = jnp.concatenate([cosine, cosine], axis=0).T * gain
        sine = jnp.concatenate([-sine, sine], axis=0).T * other_gain
        for head in range(heads):
            place = pl.ds(block * (LANES * heads) + head, LANES, stride=heads)
            cos_table[place, :] = cosine
            sin_table[place, :] = sine
        return carry

    lax.fori_loop(0, total_rows // (heads * LANES), fill, 0)

    def prepare(owner, largest):
        def body(i, largest):
            place = pl.ds(pl.multiple_of(owner * rows + i * TILE, TILE), TILE)
            x = landed[place, :].astype(jnp.float32)
            mean = jnp.sum(x * x, axis=-1, keepdims=True) * (1.0 / x.shape[-1])
            x = x * lax.rsqrt(mean + 1e-06)
            t = x * cos_table[place, :] + pltpu.roll(x, half, 1) * sin_table[place, :]
            turned[place, :] = t
            return jnp.maximum(largest, jnp.max(jnp.abs(t).reshape(TILE // 8, 8, LANES), axis=0))

        return lax.fori_loop(0, rows // TILE, body, largest)

    largest = jnp.zeros((8, LANES), jnp.float32)
    own[0].wait()
    largest = prepare(me, largest)
    for step in even[::-1]:
        for piece in range(PARTS):
            remote(0, piece, step).wait_recv()
        f, n = device(step, -1)
        largest = prepare(f * near_size + n, largest)

    head_of = lax.broadcasted_iota(jnp.int32, (8, LANES), 0) % heads
    scale = jnp.zeros((8, LANES), jnp.float32)
    for head in range(heads):
        top = jnp.max(jnp.where(head_of == head, largest, 0.0), axis=0, keepdims=True)
        out_scale[pl.ds(head, 1), :] = top
        scale = jnp.where(head_of == head, top, scale)
    inverse = (1.0 / scale)[None]

    def narrow(i, carry):
        place = pl.ds(pl.multiple_of(i * TILE, TILE), TILE)
        t = turned[place, :].reshape(TILE // 8, 8, LANES) * inverse
        out_keys[place, :] = t.reshape(TILE, LANES).astype(out_keys.dtype)
        return carry

    lax.fori_loop(0, total_rows // TILE, narrow, 0)

    own[1].wait()
    for piece in range(PARTS):
        for step in even:
            remote(1, piece, step).wait_recv()
    for which in range(2):
        for piece in range(PARTS):
            for step in even:
                remote(which, piece, step).wait_send()


def place_kernel(keys_ref, values_ref, scale_ref, out_keys, out_values, out_scale, sem):
    part = keys_ref.shape[0] // WRITES
    copies = [pltpu.make_async_copy(scale_ref, out_scale, sem.at[2, 0])]
    for i, (src, dst) in enumerate(((keys_ref, out_keys), (values_ref, out_values))):
        for j in range(WRITES):
            place = pl.ds(j * part, part)
            copies.append(pltpu.make_async_copy(src.at[place], dst.at[place], sem.at[i, j]))
    for copy in copies:
        copy.start()
    for copy in copies:
        copy.wait()


def local(far_size, near_size, raw_keys, raw_values, turn_angle, key_gain):
    sequences, positions, heads, size = raw_keys.shape
    devices = far_size * near_size
    rows = positions * heads
    total = rows * devices
    flat = (sequences, rows, size)
    whole = pltpu.VMEM((total, size), raw_keys.dtype)
    keys, values, scale = pl.pallas_call(
        functools.partial(exchange_kernel, far_size, near_size, heads),
        out_shape=(whole, whole, pltpu.VMEM((heads, size), jnp.float32)),
        in_specs=[
            pl.BlockSpec(memory_space=pl.ANY),
            pl.BlockSpec(memory_space=pl.ANY),
            pl.BlockSpec(memory_space=pl.ANY),
            pl.BlockSpec(memory_space=pl.ANY),
        ],
        out_specs=(
            pl.BlockSpec(memory_space=pltpu.VMEM),
            pl.BlockSpec(memory_space=pltpu.VMEM),
            pl.BlockSpec(memory_space=pltpu.VMEM),
        ),
        scratch_shapes=[
            pltpu.VMEM((size // 2, total // heads), jnp.float32),
            pltpu.VMEM((1, size), jnp.float32),
            pltpu.VMEM((total, size), raw_keys.dtype),
            pltpu.VMEM((total, size), jnp.float32),
            pltpu.VMEM((total, size), jnp.float32),
            pltpu.VMEM((total, size), jnp.float32),
            pltpu.SemaphoreType.DMA((2, PARTS, devices)),
            pltpu.SemaphoreType.DMA((2, PARTS, devices)),
            pltpu.SemaphoreType.DMA((4,)),
        ],
        compiler_params=pltpu.CompilerParams(
            collective_id=0, has_side_effects=True, vmem_limit_bytes=48 * 1024 * 1024
        ),
        name="exchange",
    )(raw_keys.reshape(flat), raw_values.reshape(flat), turn_angle.T, key_gain.reshape(1, size))
    out = jax.ShapeDtypeStruct((total, size), raw_keys.dtype)
    keys, values, scale = pl.pallas_call(
        place_kernel,
        out_shape=(out, out, jax.ShapeDtypeStruct((heads, size), jnp.float32)),
        in_specs=[pl.BlockSpec(memory_space=pltpu.VMEM)] * 3,
        out_specs=[pl.BlockSpec(memory_space=pl.ANY)] * 3,
        scratch_shapes=[pltpu.SemaphoreType.DMA((3, WRITES))],
        compiler_params=pltpu.CompilerParams(vmem_limit_bytes=12 * 1024 * 1024),
        name="place",
    )(keys, values, scale)
    full = (1, positions * devices, heads, size)
    return keys.reshape(full), values.reshape(full), scale.reshape(1, heads, size)


def solution(mesh):
    in_specs = (
        P(None, (FAR, NEAR), "model", None),
        P(None, (FAR, NEAR), "model", None),
        P(),
        P(),
    )
    out_specs = (
        P((FAR, NEAR), None, "model", None),
        P((FAR, NEAR), None, "model", None),
        P((FAR, NEAR), "model", None),
    )
    body = functools.partial(local, mesh.shape[FAR], mesh.shape[NEAR])
    return jax.shard_map(body, mesh=mesh, in_specs=in_specs, out_specs=out_specs, check_vma=False)
```

profile of v0, /device:TPU:0, one launch (start us, length us, event | category | flops | bytes accessed | tf_op | source)
XLA Modules:
  0.0 99.6 jit_solution(6242068583504495244)
XLA Ops:
  0.6 95.6 %exchange.1 = (bf16[16384,128]{1,0:T(8,128)(2,1)S(1)}, bf16[16384,128]{1,0:T(8,128)(2,1)S(1)}, f32[2,128]{1,0:T(2,128)S(1)}) custom-call(bf16[8,2048,128]{2,1,0:T(8,128)(2,1)} %bitcast.7, bf16[8,2048,128]{2,1,0:T(8,128)(2,1)} %bitcast.8, f32[64,8192]{1,0:T(8,128)} %bitcast.9, f32[1,128]{1,0:T(1,128)} %bitcast.10), custom_call_target="tpu_custom_call" | custom-call | tf_op jit(solution)/shard_map/exchange/pallas_call | solution.py:179
  96.2 3.4 %place.1 = (bf16[16384,128]{1,0:T(8,128)(2,1)}, bf16[16384,128]{1,0:T(8,128)(2,1)}, f32[2,128]{1,0:T(2,128)}) custom-call(bf16[16384,128]{1,0:T(8,128)(2,1)S(1)} %get-tuple-element.9.keys_ref, bf16[16384,128]{1,0:T(8,128)(2,1)S(1)} %get-tuple-element.10.values_ref, f32[2,128]{1,0:T(2,128)S(1)} %get-tuple-element.11.scale_ref), custom_call_target="tpu_custom_call" | custom-call | tf_op jit(solution)/shard_map/place/pallas_call | solution.py:210
where the time goes:
time: 99.8 us; the launch traced here: 99.6 us
  Pallas kernels  99 us (99%)
    pallas_call x1, Pallas kernels, local(): pl.pallas_call(functools.partial(exchange_kernel, far_size, near_size, he...  95.6 us
    pallas_call x1, Pallas kernels, local(): pl.pallas_call(place_kernel, out_shape=(out, out, jax.ShapeDtypeStruct((h...  3.41 us

commit v1 on v0

v1 whole, which is shorter than its diff:
```python
import functools

import jax
import jax.numpy as jnp
from jax import lax
from jax.experimental import pallas as pl
from jax.experimental.pallas import tpu as pltpu
from jax.sharding import PartitionSpec as P

FAR, NEAR = "farcp", "nearcp"
MESH_ID = pl.DeviceIdType.MESH
TILE = 256
LATE = 3
TAIL_VMEM = 51 * 1024 * 1024
WRITES = 4
LANES = 128


def step_kinds(far_size, near_size):
    kinds = {"both": [], "first": [], "second": [], "same": []}
    for step in range(1, far_size * near_size):
        far, chip = step // near_size > 0, step % near_size > 1
        kinds["both" if far and chip else "first" if far else "second" if chip else "same"].append(step)
    return kinds


def mixed(*lists):
    order = []
    for turn in range(max(map(len, lists))):
        order += [steps[turn] for steps in lists if turn < len(steps)]
    return order


def late_rows(rows):
    return rows * LATE // (4 * LANES) * LANES


def exchange_plan(far_size, near_size, rows):
    kinds = step_kinds(far_size, near_size)
    both, first, second, same = (kinds[kind] for kind in ("both", "first", "second", "same"))
    late = late_rows(rows)
    early = rows - late

    def straight(steps, parity):
        return [step for step in steps if step % 2 == parity]

    def whole(which, steps):
        return [(which, step, 0, rows) for step in steps]

    crossing = mixed(straight(first, 1), straight(second, 1), straight(both, 1)) + straight(same, 1)
    part = [(1, step, 0, early) for step in straight(both, 0)] if early else []
    rest = [(1, step, early, late) for step in straight(both, 0)]
    even = whole(0, mixed(both, first, second) + same) + part + whole(1, crossing)
    odd = whole(0, mixed(first, both, second) + same) + whole(1, crossing) + part
    odd += whole(1, mixed(straight(first, 0), straight(second, 0))) + rest
    tail = [(step, 0, rows) for step in mixed(straight(first, 0), straight(second, 0))]
    tail += [(step, early, late) for step in straight(both, 0)]
    return even, odd, tail


def position(near_size):
    return lax.axis_index(FAR) * near_size + lax.axis_index(NEAR)


def device(index, near_size):
    return {FAR: index // near_size, NEAR: index % near_size}


def greet(barrier, me, near_size, steps):
    for step in steps:
        pl.semaphore_signal(
            barrier, inc=1, device_id=device(me ^ step, near_size), device_id_type=MESH_ID
        )
    pl.semaphore_wait(barrier, len(steps))


def exchange_kernel(
    far_size, near_size, heads, keys_ref, values_ref, turn_ref, plain_gain_ref,
    out_keys, out_values, out_scale,
    angle_ref, gain_ref, landed, cos_table, sin_table, turned, send_sem, recv_sem, local_sem,
):
    me = position(near_size)
    rows = keys_ref.shape[1]
    total_rows = landed.shape[0]
    half = angle_ref.shape[0]
    devices = far_size * near_size
    even, odd, _ = exchange_plan(far_size, near_size, rows)
    slot = {copy: i for i, copy in enumerate(dict.fromkeys(even + odd))}

    angles = pltpu.make_async_copy(turn_ref, angle_ref, local_sem.at[2])
    gains = pltpu.make_async_copy(plain_gain_ref, gain_ref, local_sem.at[3])
    own = [
        pltpu.make_async_copy(src.at[me], dst.at[pl.ds(me * rows, rows)], local_sem.at[i])
        for i, (src, dst) in enumerate(((keys_ref, landed), (values_ref, out_values)))
    ]

    def remote(copy):
        which, step, offset, size = copy
        src, dst = ((keys_ref, landed), (values_ref, out_values))[which]
        return pltpu.make_async_remote_copy(
            src_ref=src.at[me ^ step, pl.ds(offset, size)],
            dst_ref=dst.at[pl.ds(me * rows + offset, size)],
            send_sem=send_sem.at[slot[copy]],
            recv_sem=recv_sem.at[slot[copy]],
            device_id=device(me ^ step, near_size),
            device_id_type=MESH_ID,
        )

    greet(pltpu.get_barrier_semaphore(), me, near_size, range(1, devices))
    for parity, copies in enumerate((even, odd)):

        @pl.when(me % 2 == parity)
        def _():
            for copy in copies:
                remote(copy).start()

    for copy in (angles, gains, *own):
        copy.start()
    angles.wait()
    gains.wait()
    gain = gain_ref[...]
    other_gain = pltpu.roll(gain, half, 1)

    def fill(block, carry):
        angle = angle_ref[:, pl.ds(pl.multiple_of(block * LANES, LANES), LANES)]
        cosine, sine = jnp.cos(angle), jnp.sin(angle)
        cosine = jnp.concatenate([cosine, cosine], axis=0).T * gain
        sine = jnp.concatenate([-sine, sine], axis=0).T * other_gain
        for head in range(heads):
            place = pl.ds(block * (LANES * heads) + head, LANES, stride=heads)
            cos_table[place, :] = cosine
            sin_table[place, :] = sine
        return carry

    lax.fori_loop(0, total_rows // (heads * LANES), fill, 0)

    def prepare(owner, largest):
        def body(i, largest):
            place = pl.ds(pl.multiple_of(owner * rows + i * TILE, TILE), TILE)
            x = landed[place, :].astype(jnp.float32)
            mean = jnp.sum(x * x, axis=-1, keepdims=True) * (1.0 / x.shape[-1])
            x = x * lax.rsqrt(mean + 1e-06)
            t = x * cos_table[place, :] + pltpu.roll(x, half, 1) * sin_table[place, :]
            turned[place, :] = t
            return jnp.maximum(largest, jnp.max(jnp.abs(t).reshape(TILE // 8, 8, LANES), axis=0))

        return lax.fori_loop(0, rows // TILE, body, largest)

    largest = jnp.zeros((8, LANES), jnp.float32)
    own[0].wait()
    largest = prepare(me, largest)
    for copy in even[devices - 2 :: -1]:
        remote(copy).wait_recv()
        largest = prepare(me ^ copy[1], largest)

    head_of = lax.broadcasted_iota(jnp.int32, (8, LANES), 0) % heads
    scale = jnp.zeros((8, LANES), jnp.float32)
    for head in range(heads):
        top = jnp.max(jnp.where(head_of == head, largest, 0.0), axis=0, keepdims=True)
        out_scale[pl.ds(head, 1), :] = top
        scale = jnp.where(head_of == head, top, scale)
    inverse = (1.0 / scale)[None]

    def narrow(i, carry):
        place = pl.ds(pl.multiple_of(i * TILE, TILE), TILE)
        t = turned[place, :].reshape(TILE // 8, 8, LANES) * inverse
        out_keys[place, :] = t.reshape(TILE, LANES).astype(out_keys.dtype)
        return carry

    lax.fori_loop(0, total_rows // TILE, narrow, 0)

    own[1].wait()
    for parity, mine, theirs in ((0, even, odd), (1, odd, even)):

        @pl.when(me % 2 == parity)
        def _():
            for copies, crossed in ((mine, 0), (theirs, 1)):
                for copy in copies:
                    if copy[0] == 1 and copy[1] % 2 == crossed:
                        remote(copy).wait_recv()
            for copy in mine:
                remote(copy).wait_send()


def tail_kernel(far_size, near_size, values_ref, after_ref, out_ref, send_sem, recv_sem):
    me = position(near_size)
    rows = values_ref.shape[1]
    plan = exchange_plan(far_size, near_size, rows)[2]

    @pl.when(me % 2 == 0)
    def _():
        greet(pltpu.get_barrier_semaphore(), me, near_size, [step for step, _, _ in plan])
        copies, place = [], 0
        for i, (step, offset, size) in enumerate(plan):
            copies.append(
                pltpu.make_async_remote_copy(
                    src_ref=values_ref.at[me ^ step, pl.ds(offset, size)],
                    dst_ref=out_ref.at[pl.ds(place, size)],
                    send_sem=send_sem.at[i],
                    recv_sem=recv_sem.at[i],
                    device_id=device(me ^ step, near_size),
                    device_id_type=MESH_ID,
                )
            )
            place += size
        for copy in copies:
            copy.start()
        for copy in copies:
            copy.wait_recv()
        for copy in copies:
            copy.wait_send()


def place_kernel(
    keys_ref, values_ref, scale_ref, out_keys, out_values, out_scale, after_ref, sem
):
    part = keys_ref.shape[0] // WRITES
    copies = [
        pltpu.make_async_copy(scale_ref, dst, sem.at[2, i]) for i, dst in enumerate((out_scale, after_ref))
    ]
    for i, (src, dst) in enumerate(((keys_ref, out_keys), (values_ref, out_values))):
        for j in range(WRITES):
            place = pl.ds(j * part, part)
            copies.append(pltpu.make_async_copy(src.at[place], dst.at[place], sem.at[i, j]))
    for copy in copies:
        copy.start()
    for copy in copies:
        copy.wait()


def place_tail_kernel(far_size, near_size, rows, values_ref, late_ref, out_ref, sem):
    me = position(near_size)

    @pl.when(me % 2 == 0)
    def _():
        copies, place = [], 0
        for i, (step, offset, size) in enumerate(exchange_plan(far_size, near_size, rows)[2]):
            copies.append(
                pltpu.make_async_copy(
                    late_ref.at[pl.ds(place, size)],
                    out_ref.at[pl.ds((me ^ step) * rows + offset, size)],
                    sem.at[i],
                )
            )
            place += size
        for copy in copies:
            copy.start()
        for copy in copies:
            copy.wait()


def local(far_size, near_size, raw_keys, raw_values, turn_angle, key_gain):
    sequences, positions, heads, size = raw_keys.shape
    devices = far_size * near_size
    rows = positions * heads
    total = rows * devices
    flat = (sequences, rows, size)
    even, odd, tail = exchange_plan(far_size, near_size, rows)
    raw_values = raw_values.reshape(flat)
    whole = pltpu.VMEM((total, size), raw_keys.dtype)
    keys, values, scale = pl.pallas_call(
        functools.partial(exchange_kernel, far_size, near_size, heads),
        out_shape=(whole, whole, pltpu.VMEM((heads, size), jnp.float32)),
        in_specs=[
            pl.BlockSpec(memory_space=pl.ANY),
            pl.BlockSpec(memory_space=pl.ANY),
            pl.BlockSpec(memory_space=pl.ANY),
            pl.BlockSpec(memory_space=pl.ANY),
        ],
        out_specs=(
            pl.BlockSpec(memory_space=pltpu.VMEM),
            pl.BlockSpec(memory_space=pltpu.VMEM),
            pl.BlockSpec(memory_space=pltpu.VMEM),
        ),
        scratch_shapes=[
            pltpu.VMEM((size // 2, total // heads), jnp.float32),
            pltpu.VMEM((1, size), jnp.float32),
            pltpu.VMEM((total, size), raw_keys.dtype),
            pltpu.VMEM((total, size), jnp.float32),
            pltpu.VMEM((total, size), jnp.float32),
            pltpu.VMEM((total, size), jnp.float32),
            pltpu.SemaphoreType.DMA((len(set(even + odd)),)),
            pltpu.SemaphoreType.DMA((len(set(even + odd)),)),
            pltpu.SemaphoreType.DMA((4,)),
        ],
        compiler_params=pltpu.CompilerParams(
            collective_id=0, has_side_effects=True, vmem_limit_bytes=48 * 1024 * 1024
        ),
        name="exchange",
    )(raw_keys.reshape(flat), raw_values, turn_angle.T, key_gain.reshape(1, size))
    out = jax.ShapeDtypeStruct((total, size), raw_keys.dtype)
    in_vmem = pl.BlockSpec(memory_space=pltpu.VMEM)
    anywhere = pl.BlockSpec(memory_space=pl.ANY)
    keys, values, scale, after = pl.pallas_call(
        place_kernel,
        out_shape=(
            out, out, jax.ShapeDtypeStruct((heads, size), jnp.float32),
            jax.ShapeDtypeStruct((heads, size), jnp.float32),
        ),
        in_specs=[in_vmem] * 3,
        out_specs=[anywhere] * 4,
        scratch_shapes=[pltpu.SemaphoreType.DMA((3, WRITES))],
        compiler_params=pltpu.CompilerParams(vmem_limit_bytes=12 * 1024 * 1024),
        name="place",
    )(keys, values, scale)
    late = pl.pallas_call(
        functools.partial(tail_kernel, far_size, near_size),
        out_shape=pltpu.VMEM((sum(copy[2] for copy in tail), size), raw_keys.dtype),
        in_specs=[anywhere, anywhere],
        out_specs=in_vmem,
        scratch_shapes=[pltpu.SemaphoreType.DMA((len(tail),))] * 2,
        compiler_params=pltpu.CompilerParams(
            collective_id=1, has_side_effects=True, vmem_limit_bytes=TAIL_VMEM
        ),
        name="tail",
    )(raw_values, after)
    values = pl.pallas_call(
        functools.partial(place_tail_kernel, far_size, near_size, rows),
        out_shape=out,
        in_specs=[anywhere, in_vmem],
        out_specs=anywhere,
        input_output_aliases={0: 0},
        scratch_shapes=[pltpu.SemaphoreType.DMA((len(tail),))],
        compiler_params=pltpu.CompilerParams(vmem_limit_bytes=12 * 1024 * 1024),
        name="place_tail",
    )(values, late)
    full = (1, positions * devices, heads, size)
    return keys.reshape(full), values.reshape(full), scale.reshape(1, heads, size)


def solution(mesh):
    in_specs = (
        P(None, (FAR, NEAR), "model", None),
        P(None, (FAR, NEAR), "model", None),
        P(),
        P(),
    )
    out_specs = (
        P((FAR, NEAR), None, "model", None),
        P((FAR, NEAR), None, "model", None),
        P((FAR, NEAR), "model", None),
    )
    body = functools.partial(local, mesh.shape[FAR], mesh.shape[NEAR])
    return jax.shard_map(body, mesh=mesh, in_specs=in_specs, out_specs=out_specs, check_vma=False)
```

time: 99.8 us -> 97.7 us (0.979)
  Pallas kernels: 99 us -> 96.9 us
    pallas_call x1, Pallas kernels: 95.6 us -> 76.1 us  [local(): pl.pallas_call(functools.partial(exchange_kernel, far_size, near_size, he...]
    pallas_call x0 -> x2, Pallas kernels: none -> 17.4 us  [the longest x1 16.3 us: local(): pl.pallas_call(functools.partial(tail_kernel, far_size, near_size), out_s...]
where the time goes in v1:
time: 97.7 us; the launch traced here: 97.6 us
  Pallas kernels  96.9 us (99%)
    pallas_call x1, Pallas kernels, local(): pl.pallas_call(functools.partial(exchange_kernel, far_size, near_size, he...  76.1 us
    pallas_call x1, Pallas kernels, local(): pl.pallas_call(functools.partial(tail_kernel, far_size, near_size), out_s...  16.3 us
    pallas_call x1, Pallas kernels, local(): pl.pallas_call(place_kernel, out_shape=(out, out, jax.ShapeDtypeStruct((h...  3.41 us

profile of v1, /device:TPU:0, one launch (start us, length us, event | category | flops | bytes accessed | tf_op | source)
XLA Modules:
  0.0 97.6 jit_solution(9781529739046717756)
XLA Ops:
  0.6 76.1 %exchange.1 = (bf16[16384,128]{1,0:T(8,128)(2,1)S(1)}, bf16[16384,128]{1,0:T(8,128)(2,1)S(1)}, f32[2,128]{1,0:T(2,128)S(1)}) custom-call(bf16[8,2048,128]{2,1,0:T(8,128)(2,1)} %bitcast.10, bf16[8,2048,128]{2,1,0:T(8,128)(2,1)} %bitcast.7, f32[64,8192]{1,0:T(8,128)} %bitcast.11, f32[1,128]{1,0:T(1,128)} %bitcast.12), custom_call_target="tpu_custom_call" | custom-call | tf_op jit(solution)/shard_map/exchange/pallas_call | solution.py:261
  76.7 3.4 %place.1 = (bf16[16384,128]{1,0:T(8,128)(2,1)}, bf16[16384,128]{1,0:T(8,128)(2,1)}, f32[2,128]{1,0:T(2,128)}, f32[2,128]{1,0:T(2,128)S(1)}) custom-call(bf16[16384,128]{1,0:T(8,128)(2,1)S(1)} %get-tuple-element.10.keys_ref, bf16[16384,128]{1,0:T(8,128)(2,1)S(1)} %get-tuple-element.11.values_ref, f32[2,128]{1,0:T(2,128)S(1)} %get-tuple-element.12.scale_ref), custom_call_target="tpu_custom_call" | custom-call | tf_op jit(solution)/shard_map/place/pallas_call | solution.py:294
  80.2 16.3 %tail.1.late_ref = bf16[5632,128]{1,0:T(8,128)(2,1)S(1)} custom-call(bf16[8,2048,128]{2,1,0:T(8,128)(2,1)} %bitcast.8, f32[2,128]{1,0:T(2,128)S(1)} %get-tuple-element.15.after_ref), custom_call_target="tpu_custom_call" | custom-call | tf_op jit(solution)/shard_map/tail/pallas_call | solution.py:306
  96.4 1.1 %place_tail.1 = bf16[16384,128]{1,0:T(8,128)(2,1)} custom-call(bf16[16384,128]{1,0:T(8,128)(2,1)} %get-tuple-element.14.values_ref, bf16[5632,128]{1,0:T(8,128)(2,1)S(1)} %tail.1.late_ref), custom_call_target="tpu_custom_call", output_to_operand_aliasing={{}: (0, {})} | custom-call | tf_op jit(solution)/shard_map/place_tail/pallas_call | solution.py:317

commit v2 on v1

--- a/solution.py
+++ b/solution.py
@@ -10,7 +10,8 @@
 FAR, NEAR = "farcp", "nearcp"
 MESH_ID = pl.DeviceIdType.MESH
 TILE = 256
-LATE = 3
+LATE = 14
+LAST = 3
 TAIL_VMEM = 51 * 1024 * 1024
 WRITES = 4
 LANES = 128
@@ -32,7 +33,7 @@
 
 
 def late_rows(rows):
-    return rows * LATE // (4 * LANES) * LANES
+    return rows * LATE // (16 * LANES) * LANES
 
 
 def exchange_plan(far_size, near_size, rows):
@@ -50,12 +51,17 @@
     crossing = mixed(straight(first, 1), straight(second, 1), straight(both, 1)) + straight(same, 1)
     part = [(1, step, 0, early) for step in straight(both, 0)] if early else []
     rest = [(1, step, early, late) for step in straight(both, 0)]
-    even = whole(0, mixed(both, first, second) + same) + part + whole(1, crossing)
-    odd = whole(0, mixed(first, both, second) + same) + whole(1, crossing) + part
+    last = LAST * LANES
+    even = whole(0, second + mixed(both, first) + same) + part
+    even += [(1, step, 0, last) for step in straight(second, 0)] + whole(1, crossing)
+    odd = whole(0, second + mixed(first, both) + same) + whole(1, crossing) + part
     odd += whole(1, mixed(straight(first, 0), straight(second, 0))) + rest
-    tail = [(step, 0, rows) for step in mixed(straight(first, 0), straight(second, 0))]
-    tail += [(step, early, late) for step in straight(both, 0)]
-    return even, odd, tail
+    corner = mixed(
+        [(step, 0, rows - last) for step in straight(first, 0)],
+        [(step, last, rows - last) for step in straight(second, 0)],
+    )
+    corner += [(step, early, late) for step in straight(both, 0)]
+    return even, odd, corner + [(step, rows - last, last) for step in straight(first, 0)]
 
 
 def position(near_size):
@@ -66,18 +72,33 @@
     return {FAR: index // near_size, NEAR: index % near_size}
 
 
+def signal(semaphore, index, near_size):
+    pl.semaphore_signal(
+        semaphore, inc=1, device_id=device(index, near_size), device_id_type=MESH_ID
+    )
+
+
 def greet(barrier, me, near_size, steps):
     for step in steps:
-        pl.semaphore_signal(
-            barrier, inc=1, device_id=device(me ^ step, near_size), device_id_type=MESH_ID
-        )
+        signal(barrier, me ^ step, near_size)
     pl.semaphore_wait(barrier, len(steps))
+
+
+def greet_upwards(barrier, ready, me, near_size, steps):
+    below = 0
+    for step in steps:
+        below += jnp.where((me & step) == step, 1, 0)
+        pl.when((me & step) == 0)(functools.partial(signal, barrier, me ^ step, near_size))
+    pl.when(me > 0)(functools.partial(pl.semaphore_wait, barrier, below))
+    for step in steps:
+        answer = functools.partial(signal, ready.at[step], me ^ step, near_size)
+        pl.when((me & step) == step)(answer)
 
 
 def exchange_kernel(
     far_size, near_size, heads, keys_ref, values_ref, turn_ref, plain_gain_ref,
     out_keys, out_values, out_scale,
-    angle_ref, gain_ref, landed, cos_table, sin_table, turned, send_sem, recv_sem, local_sem,
+    angle_ref, gain_ref, landed, cos_table, sin_table, turned, send_sem, recv_sem, ready, local_sem,
 ):
     me = position(near_size)
     rows = keys_ref.shape[1]
@@ -106,12 +127,28 @@
             device_id_type=MESH_ID,
         )
 
-    greet(pltpu.get_barrier_semaphore(), me, near_size, range(1, devices))
+    kinds = step_kinds(far_size, near_size)
+    stages = (kinds["second"] + kinds["same"], kinds["first"], kinds["both"])
+    greet_upwards(pltpu.get_barrier_semaphore(), ready, me, near_size, sum(stages, []))
+
+    def wait_ready(steps):
+        for step in steps:
+            wait = functools.partial(pl.semaphore_wait, ready.at[step], 1)
+            pl.when((me & step) == 0)(wait)
+
+    wait_ready(stages[0])
+    for step in kinds["second"]:
+        remote((0, step, 0, rows)).start()
     for parity, copies in enumerate((even, odd)):
 
         @pl.when(me % 2 == parity)
         def _():
-            for copy in copies:
+            waited = 1
+            for copy in copies[len(kinds["second"]) :]:
+                stage = [i for i, steps in enumerate(stages) if copy[1] in steps][0]
+                for i in range(waited, stage + 1):
+                    wait_ready(stages[i])
+                waited = max(waited, stage + 1)
                 remote(copy).start()
 
     for copy in (angles, gains, *own):
@@ -189,10 +226,10 @@
 
     @pl.when(me % 2 == 0)
     def _():
-        greet(pltpu.get_barrier_semaphore(), me, near_size, [step for step, _, _ in plan])
-        copies, place = [], 0
+        greet(pltpu.get_barrier_semaphore(), me, near_size, sorted({step for step, _, _ in plan}))
+        copies, place = {}, 0
         for i, (step, offset, size) in enumerate(plan):
-            copies.append(
+            copies[step, offset] = (
                 pltpu.make_async_remote_copy(
                     src_ref=values_ref.at[me ^ step, pl.ds(offset, size)],
                     dst_ref=out_ref.at[pl.ds(place, size)],
@@ -203,11 +240,20 @@
                 )
             )
             place += size
-        for copy in copies:
-            copy.start()
-        for copy in copies:
+        kinds = step_kinds(far_size, near_size)
+        inner = [copy for copy in plan if copy[0] not in kinds["both"]]
+        outer = [copy for copy in plan if copy[0] in kinds["both"]]
+        bent = me == near_size
+        for order, here in ((inner + outer, bent), (plan, ~bent)):
+
+            @pl.when(here)
+            def _():
+                for step, offset, _ in order:
+                    copies[step, offset].start()
+
+        for copy in copies.values():
             copy.wait_recv()
-        for copy in copies:
+        for copy in copies.values():
             copy.wait_send()
 
 
@@ -281,6 +327,7 @@
             pltpu.VMEM((total, size), jnp.float32),
             pltpu.SemaphoreType.DMA((len(set(even + odd)),)),
             pltpu.SemaphoreType.DMA((len(set(even + odd)),)),
+            pltpu.SemaphoreType.REGULAR((devices,)),
             pltpu.SemaphoreType.DMA((4,)),
         ],
         compiler_params=pltpu.CompilerParams(

time: 97.7 us -> 96.7 us (0.990)
  Pallas kernels: 96.9 us -> 95.9 us
where the time goes in v2:
time: 96.7 us; the launch traced here: 96.5 us
  Pallas kernels  95.9 us (99%)
    pallas_call x1, Pallas kernels, local(): pl.pallas_call(functools.partial(exchange_kernel, far_size, near_size, he...  75.7 us
    pallas_call x1, Pallas kernels, local(): pl.pallas_call(functools.partial(tail_kernel, far_size, near_size), out_s...  15.6 us
    pallas_call x1, Pallas kernels, local(): pl.pallas_call(place_kernel, out_shape=(out, out, jax.ShapeDtypeStruct((h...  3.41 us

profile of v2, /device:TPU:0, one launch (start us, length us, event | category | flops | bytes accessed | tf_op | source)
XLA Modules:
  0.0 96.5 jit_solution(11963937808296051093)
XLA Ops:
  0.6 75.7 %exchange.1 = (bf16[16384,128]{1,0:T(8,128)(2,1)S(1)}, bf16[16384,128]{1,0:T(8,128)(2,1)S(1)}, f32[2,128]{1,0:T(2,128)S(1)}) custom-call(bf16[8,2048,128]{2,1,0:T(8,128)(2,1)} %bitcast.10, bf16[8,2048,128]{2,1,0:T(8,128)(2,1)} %bitcast.7, f32[64,8192]{1,0:T(8,128)} %bitcast.11, f32[1,128]{1,0:T(1,128)} %bitcast.12), custom_call_target="tpu_custom_call" | custom-call | tf_op jit(solution)/shard_map/exchange/pallas_call | solution.py:307
  76.4 3.4 %place.1 = (bf16[16384,128]{1,0:T(8,128)(2,1)}, bf16[16384,128]{1,0:T(8,128)(2,1)}, f32[2,128]{1,0:T(2,128)}, f32[2,128]{1,0:T(2,128)S(1)}) custom-call(bf16[16384,128]{1,0:T(8,128)(2,1)S(1)} %get-tuple-element.10.keys_ref, bf16[16384,128]{1,0:T(8,128)(2,1)S(1)} %get-tuple-element.11.values_ref, f32[2,128]{1,0:T(2,128)S(1)} %get-tuple-element.12.scale_ref), custom_call_target="tpu_custom_call" | custom-call | tf_op jit(solution)/shard_map/place/pallas_call | solution.py:341
  79.8 15.6 %tail.1.late_ref = bf16[5504,128]{1,0:T(8,128)(2,1)S(1)} custom-call(bf16[8,2048,128]{2,1,0:T(8,128)(2,1)} %bitcast.8, f32[2,128]{1,0:T(2,128)S(1)} %get-tuple-element.15.after_ref), custom_call_target="tpu_custom_call" | custom-call | tf_op jit(solution)/shard_map/tail/pallas_call | solution.py:353
  95.4 1.1 %place_tail.1 = bf16[16384,128]{1,0:T(8,128)(2,1)} custom-call(bf16[16384,128]{1,0:T(8,128)(2,1)} %get-tuple-element.14.values_ref, bf16[5504,128]{1,0:T(8,128)(2,1)S(1)} %tail.1.late_ref), custom_call_target="tpu_custom_call", output_to_operand_aliasing={{}: (0, {})} | custom-call | tf_op jit(solution)/shard_map/place_tail/pallas_call | solution.py:364

commit v3 on v2

--- a/solution.py
+++ b/solution.py
@@ -10,8 +10,10 @@
 FAR, NEAR = "farcp", "nearcp"
 MESH_ID = pl.DeviceIdType.MESH
 TILE = 256
-LATE = 14
-LAST = 3
+LATE = 15
+HEAD = 2
+LAST = 4
+MOVED = 4
 TAIL_VMEM = 51 * 1024 * 1024
 WRITES = 4
 LANES = 128
@@ -46,19 +48,24 @@
         return [step for step in steps if step % 2 == parity]
 
     def whole(which, steps):
-        return [(which, step, 0, rows) for step in steps]
+        copies = []
+        for step in steps:
+            head = HEAD * LANES if which == 0 and step == near_size else 0
+            copies += [(which, step, 0, head)] if head else []
+            copies.append((which, step, head, rows - head))
+        return copies
 
     crossing = mixed(straight(first, 1), straight(second, 1), straight(both, 1)) + straight(same, 1)
     part = [(1, step, 0, early) for step in straight(both, 0)] if early else []
     rest = [(1, step, early, late) for step in straight(both, 0)]
-    last = LAST * LANES
+    last, moved = LAST * LANES, MOVED * LANES
     even = whole(0, second + mixed(both, first) + same) + part
-    even += [(1, step, 0, last) for step in straight(second, 0)] + whole(1, crossing)
+    even += [(1, step, 0, moved) for step in straight(second, 0)] + whole(1, crossing)
     odd = whole(0, second + mixed(first, both) + same) + whole(1, crossing) + part
     odd += whole(1, mixed(straight(first, 0), straight(second, 0))) + rest
     corner = mixed(
         [(step, 0, rows - last) for step in straight(first, 0)],
-        [(step, last, rows - last) for step in straight(second, 0)],
+        [(step, moved, rows - moved) for step in straight(second, 0)],
     )
     corner += [(step, early, late) for step in straight(both, 0)]
     return even, odd, corner + [(step, rows - last, last) for step in straight(first, 0)]
@@ -136,20 +143,27 @@
             wait = functools.partial(pl.semaphore_wait, ready.at[step], 1)
             pl.when((me & step) == 0)(wait)
 
+    head = (0, near_size, 0, HEAD * LANES)
+    chip, turn = me // 2, near_size // 2
+    before = chip == turn
+    between = chip == 0
+
+    pl.when(before)(remote(head).start)
     wait_ready(stages[0])
     for step in kinds["second"]:
         remote((0, step, 0, rows)).start()
+    wait_ready(stages[1])
+    pl.when(between)(remote(head).start)
+    wait_ready(stages[2])
     for parity, copies in enumerate((even, odd)):
 
         @pl.when(me % 2 == parity)
         def _():
-            waited = 1
             for copy in copies[len(kinds["second"]) :]:
-                stage = [i for i, steps in enumerate(stages) if copy[1] in steps][0]
-                for i in range(waited, stage + 1):
-                    wait_ready(stages[i])
-                waited = max(waited, stage + 1)
-                remote(copy).start()
+                if copy == head:
+                    pl.when(~(before | between))(remote(copy).start)
+                else:
+                    remote(copy).start()
 
     for copy in (angles, gains, *own):
         copy.start()
@@ -186,9 +200,11 @@
     largest = jnp.zeros((8, LANES), jnp.float32)
     own[0].wait()
     largest = prepare(me, largest)
-    for copy in even[devices - 2 :: -1]:
-        remote(copy).wait_recv()
-        largest = prepare(me ^ copy[1], largest)
+    remote(head).wait_recv()
+    for copy in even[devices - 1 :: -1]:
+        if copy != head:
+            remote(copy).wait_recv()
+            largest = prepare(me ^ copy[1], largest)
 
     head_of = lax.broadcasted_iota(jnp.int32, (8, LANES), 0) % heads
     scale = jnp.zeros((8, LANES), jnp.float32)

time: 96.7 us -> 96.5 us (level)
  no operation moved by 1% of the time
where the time goes in v3:
time: 96.5 us; the launch traced here: 96.4 us
  Pallas kernels  95.7 us (99%)
    pallas_call x1, Pallas kernels, local(): pl.pallas_call(functools.partial(exchange_kernel, far_size, near_size, he...  75.9 us
    pallas_call x1, Pallas kernels, local(): pl.pallas_call(functools.partial(tail_kernel, far_size, near_size), out_s...  15.3 us
    pallas_call x1, Pallas kernels, local(): pl.pallas_call(place_kernel, out_shape=(out, out, jax.ShapeDtypeStruct((h...  3.41 us

profile of v3, /device:TPU:0, one launch (start us, length us, event | category | flops | bytes accessed | tf_op | source)
XLA Modules:
  0.0 96.4 jit_solution(16100319880812524700)
XLA Ops:
  0.6 75.9 %exchange.1 = (bf16[16384,128]{1,0:T(8,128)(2,1)S(1)}, bf16[16384,128]{1,0:T(8,128)(2,1)S(1)}, f32[2,128]{1,0:T(2,128)S(1)}) custom-call(bf16[8,2048,128]{2,1,0:T(8,128)(2,1)} %bitcast.10, bf16[8,2048,128]{2,1,0:T(8,128)(2,1)} %bitcast.7, f32[64,8192]{1,0:T(8,128)} %bitcast.11, f32[1,128]{1,0:T(1,128)} %bitcast.12), custom_call_target="tpu_custom_call" | custom-call | tf_op jit(solution)/shard_map/exchange/pallas_call | solution.py:323
  76.5 3.4 %place.1 = (bf16[16384,128]{1,0:T(8,128)(2,1)}, bf16[16384,128]{1,0:T(8,128)(2,1)}, f32[2,128]{1,0:T(2,128)}, f32[2,128]{1,0:T(2,128)S(1)}) custom-call(bf16[16384,128]{1,0:T(8,128)(2,1)S(1)} %get-tuple-element.10.keys_ref, bf16[16384,128]{1,0:T(8,128)(2,1)S(1)} %get-tuple-element.11.values_ref, f32[2,128]{1,0:T(2,128)S(1)} %get-tuple-element.12.scale_ref), custom_call_target="tpu_custom_call" | custom-call | tf_op jit(solution)/shard_map/place/pallas_call | solution.py:357
  80.0 15.3 %tail.1.late_ref = bf16[5504,128]{1,0:T(8,128)(2,1)S(1)} custom-call(bf16[8,2048,128]{2,1,0:T(8,128)(2,1)} %bitcast.8, f32[2,128]{1,0:T(2,128)S(1)} %get-tuple-element.15.after_ref), custom_call_target="tpu_custom_call" | custom-call | tf_op jit(solution)/shard_map/tail/pallas_call | solution.py:369
  95.2 1.1 %place_tail.1 = bf16[16384,128]{1,0:T(8,128)(2,1)} custom-call(bf16[16384,128]{1,0:T(8,128)(2,1)} %get-tuple-element.14.values_ref, bf16[5504,128]{1,0:T(8,128)(2,1)S(1)} %tail.1.late_ref), custom_call_target="tpu_custom_call", output_to_operand_aliasing={{}: (0, {})} | custom-call | tf_op jit(solution)/shard_map/place_tail/pallas_call | solution.py:380

commit v4 on v3

--- a/solution.py
+++ b/solution.py
@@ -10,7 +10,8 @@
 FAR, NEAR = "farcp", "nearcp"
 MESH_ID = pl.DeviceIdType.MESH
 TILE = 256
-LATE = 15
+LATE = 14
+RELAY = 64
 HEAD = 2
 LAST = 4
 MOVED = 4
@@ -36,6 +37,10 @@
 
 def late_rows(rows):
     return rows * LATE // (16 * LANES) * LANES
+
+
+def relayed_copy(near_size):
+    return (1, near_size + 2, 0, RELAY)
 
 
 def exchange_plan(far_size, near_size, rows):
@@ -56,7 +61,10 @@
         return copies
 
     crossing = mixed(straight(first, 1), straight(second, 1), straight(both, 1)) + straight(same, 1)
-    part = [(1, step, 0, early) for step in straight(both, 0)] if early else []
+    part = [relayed_copy(near_size)]
+    for step in straight(both, 0):
+        skip = RELAY if step == part[0][1] else 0
+        part.append((1, step, skip, early - skip))
     rest = [(1, step, early, late) for step in straight(both, 0)]
     last, moved = LAST * LANES, MOVED * LANES
     even = whole(0, second + mixed(both, first) + same) + part
@@ -105,7 +113,8 @@
 def exchange_kernel(
     far_size, near_size, heads, keys_ref, values_ref, turn_ref, plain_gain_ref,
     out_keys, out_values, out_scale,
-    angle_ref, gain_ref, landed, cos_table, sin_table, turned, send_sem, recv_sem, ready, local_sem,
+    angle_ref, gain_ref, landed, cos_table, sin_table, turned, held,
+    send_sem, recv_sem, relay_sem, ready, local_sem,
 ):
     me = position(near_size)
     rows = keys_ref.shape[1]
@@ -148,8 +157,28 @@
     before = chip == turn
     between = chip == 0
 
+    relayed = relayed_copy(near_size)
+    to_relay = pltpu.make_async_remote_copy(
+        src_ref=values_ref.at[me ^ relayed[1], pl.ds(0, RELAY)],
+        dst_ref=held,
+        send_sem=relay_sem.at[0],
+        recv_sem=relay_sem.at[1],
+        device_id=device(me ^ 2, near_size),
+        device_id_type=MESH_ID,
+    )
+    from_relay = pltpu.make_async_remote_copy(
+        src_ref=held,
+        dst_ref=out_values.at[pl.ds((me ^ 2) * rows, RELAY)],
+        send_sem=relay_sem.at[2],
+        recv_sem=recv_sem.at[slot[relayed]],
+        device_id=device(me ^ near_size, near_size),
+        device_id_type=MESH_ID,
+    )
+    source, relay = chip == turn + 1, chip == turn
+
     pl.when(before)(remote(head).start)
     wait_ready(stages[0])
+    pl.when(source)(to_relay.start)
     for step in kinds["second"]:
         remote((0, step, 0, rows)).start()
     wait_ready(stages[1])
@@ -162,6 +191,14 @@
             for copy in copies[len(kinds["second"]) :]:
                 if copy == head:
                     pl.when(~(before | between))(remote(copy).start)
+                elif copy == relayed:
+
+                    @pl.when(relay)
+                    def _():
+                        to_relay.wait_recv()
+                        from_relay.start()
+
+                    pl.when(~source)(remote(copy).start)
                 else:
                     remote(copy).start()
 
@@ -232,7 +269,12 @@
                     if copy[0] == 1 and copy[1] % 2 == crossed:
                         remote(copy).wait_recv()
             for copy in mine:
-                remote(copy).wait_send()
+                if copy == relayed:
+                    pl.when(source)(to_relay.wait_send)
+                    pl.when(relay)(from_relay.wait_send)
+                    pl.when(~source)(remote(copy).wait_send)
+                else:
+                    remote(copy).wait_send()
 
 
 def tail_kernel(far_size, near_size, values_ref, after_ref, out_ref, send_sem, recv_sem):
@@ -341,8 +383,10 @@
             pltpu.VMEM((total, size), jnp.float32),
             pltpu.VMEM((total, size), jnp.float32),
             pltpu.VMEM((total, size), jnp.float32),
+            pltpu.VMEM((RELAY, size), raw_keys.dtype),
             pltpu.SemaphoreType.DMA((len(set(even + odd)),)),
             pltpu.SemaphoreType.DMA((len(set(even + odd)),)),
+            pltpu.SemaphoreType.DMA((3,)),
             pltpu.SemaphoreType.REGULAR((devices,)),
             pltpu.SemaphoreType.DMA((4,)),
         ],

time: 96.5 us -> 96.4 us (level)
  no operation moved by 1% of the time
where the time goes in v4:
time: 96.4 us; the launch traced here: 96.3 us
  Pallas kernels  95.6 us (99%)
    pallas_call x1, Pallas kernels, local(): pl.pallas_call(functools.partial(exchange_kernel, far_size, near_size, he...  76.7 us
    pallas_call x1, Pallas kernels, local(): pl.pallas_call(functools.partial(tail_kernel, far_size, near_size), out_s...  14.4 us
    pallas_call x1, Pallas kernels, local(): pl.pallas_call(place_kernel, out_shape=(out, out, jax.ShapeDtypeStruct((h...  3.41 us

profile of v4, /device:TPU:0, one launch (start us, length us, event | category | flops | bytes accessed | tf_op | source)
XLA Modules:
  0.0 96.3 jit_solution(18425485307163243798)
XLA Ops:
  0.6 76.7 %exchange.1 = (bf16[16384,128]{1,0:T(8,128)(2,1)S(1)}, bf16[16384,128]{1,0:T(8,128)(2,1)S(1)}, f32[2,128]{1,0:T(2,128)S(1)}) custom-call(bf16[8,2048,128]{2,1,0:T(8,128)(2,1)} %bitcast.10, bf16[8,2048,128]{2,1,0:T(8,128)(2,1)} %bitcast.7, f32[64,8192]{1,0:T(8,128)} %bitcast.11, f32[1,128]{1,0:T(1,128)} %bitcast.12), custom_call_target="tpu_custom_call" | custom-call | tf_op jit(solution)/shard_map/exchange/pallas_call | solution.py:365
  77.3 3.4 %place.1 = (bf16[16384,128]{1,0:T(8,128)(2,1)}, bf16[16384,128]{1,0:T(8,128)(2,1)}, f32[2,128]{1,0:T(2,128)}, f32[2,128]{1,0:T(2,128)S(1)}) custom-call(bf16[16384,128]{1,0:T(8,128)(2,1)S(1)} %get-tuple-element.10.keys_ref, bf16[16384,128]{1,0:T(8,128)(2,1)S(1)} %get-tuple-element.11.values_ref, f32[2,128]{1,0:T(2,128)S(1)} %get-tuple-element.12.scale_ref), custom_call_target="tpu_custom_call" | custom-call | tf_op jit(solution)/shard_map/place/pallas_call | solution.py:401
  80.7 14.4 %tail.1.late_ref = bf16[5376,128]{1,0:T(8,128)(2,1)S(1)} custom-call(bf16[8,2048,128]{2,1,0:T(8,128)(2,1)} %bitcast.8, f32[2,128]{1,0:T(2,128)S(1)} %get-tuple-element.15.after_ref), custom_call_target="tpu_custom_call" | custom-call | tf_op jit(solution)/shard_map/tail/pallas_call | solution.py:413
  95.1 1.1 %place_tail.1 = bf16[16384,128]{1,0:T(8,128)(2,1)} custom-call(bf16[16384,128]{1,0:T(8,128)(2,1)} %get-tuple-element.14.values_ref, bf16[5376,128]{1,0:T(8,128)(2,1)S(1)} %tail.1.late_ref), custom_call_target="tpu_custom_call", output_to_operand_aliasing={{}: (0, {})} | custom-call | tf_op jit(solution)/shard_map/place_tail/pallas_call | solution.py:424

commit v5 on v4

--- a/solution.py
+++ b/solution.py
@@ -13,8 +13,8 @@
 LATE = 14
 RELAY = 64
 HEAD = 2
-LAST = 4
-MOVED = 4
+LAST = 3
+MOVED = 3
 TAIL_VMEM = 51 * 1024 * 1024
 WRITES = 4
 LANES = 128

time: 96.4 us -> 96.4 us (level)
  no operation moved by 1% of the time
where the time goes in v5:
time: 96.4 us; the launch traced here: 96.2 us
  Pallas kernels  95.5 us (99%)
    pallas_call x1, Pallas kernels, local(): pl.pallas_call(functools.partial(exchange_kernel, far_size, near_size, he...  75.9 us
    pallas_call x1, Pallas kernels, local(): pl.pallas_call(functools.partial(tail_kernel, far_size, near_size), out_s...  15.1 us
    pallas_call x1, Pallas kernels, local(): pl.pallas_call(place_kernel, out_shape=(out, out, jax.ShapeDtypeStruct((h...  3.41 us

profile of v5, /device:TPU:0, one launch (start us, length us, event | category | flops | bytes accessed | tf_op | source)
XLA Modules:
  0.0 96.2 jit_solution(1064554903407293679)
XLA Ops:
  0.6 75.9 %exchange.1 = (bf16[16384,128]{1,0:T(8,128)(2,1)S(1)}, bf16[16384,128]{1,0:T(8,128)(2,1)S(1)}, f32[2,128]{1,0:T(2,128)S(1)}) custom-call(bf16[8,2048,128]{2,1,0:T(8,128)(2,1)} %bitcast.10, bf16[8,2048,128]{2,1,0:T(8,128)(2,1)} %bitcast.7, f32[64,8192]{1,0:T(8,128)} %bitcast.11, f32[1,128]{1,0:T(1,128)} %bitcast.12), custom_call_target="tpu_custom_call" | custom-call | tf_op jit(solution)/shard_map/exchange/pallas_call | solution.py:365
  76.6 3.4 %place.1 = (bf16[16384,128]{1,0:T(8,128)(2,1)}, bf16[16384,128]{1,0:T(8,128)(2,1)}, f32[2,128]{1,0:T(2,128)}, f32[2,128]{1,0:T(2,128)S(1)}) custom-call(bf16[16384,128]{1,0:T(8,128)(2,1)S(1)} %get-tuple-element.10.keys_ref, bf16[16384,128]{1,0:T(8,128)(2,1)S(1)} %get-tuple-element.11.values_ref, f32[2,128]{1,0:T(2,128)S(1)} %get-tuple-element.12.scale_ref), custom_call_target="tpu_custom_call" | custom-call | tf_op jit(solution)/shard_map/place/pallas_call | solution.py:401
  80.0 15.1 %tail.1.late_ref = bf16[5504,128]{1,0:T(8,128)(2,1)S(1)} custom-call(bf16[8,2048,128]{2,1,0:T(8,128)(2,1)} %bitcast.8, f32[2,128]{1,0:T(2,128)S(1)} %get-tuple-element.15.after_ref), custom_call_target="tpu_custom_call" | custom-call | tf_op jit(solution)/shard_map/tail/pallas_call | solution.py:413
  95.1 1.1 %place_tail.1 = bf16[16384,128]{1,0:T(8,128)(2,1)} custom-call(bf16[16384,128]{1,0:T(8,128)(2,1)} %get-tuple-element.14.values_ref, bf16[5504,128]{1,0:T(8,128)(2,1)S(1)} %tail.1.late_ref), custom_call_target="tpu_custom_call", output_to_operand_aliasing={{}: (0, {})} | custom-call | tf_op jit(solution)/shard_map/place_tail/pallas_call | solution.py:424

commit v6 on v4

--- a/solution.py
+++ b/solution.py
@@ -12,7 +12,7 @@
 TILE = 256
 LATE = 14
 RELAY = 64
-HEAD = 2
+HEAD = 3
 LAST = 4
 MOVED = 4
 TAIL_VMEM = 51 * 1024 * 1024

time: 96.4 us -> 96.4 us (level)
  no operation moved by 1% of the time
where the time goes in v6:
time: 96.4 us; the launch traced here: 96.3 us
  Pallas kernels  95.6 us (99%)
    pallas_call x1, Pallas kernels, local(): pl.pallas_call(functools.partial(exchange_kernel, far_size, near_size, he...  76.7 us
    pallas_call x1, Pallas kernels, local(): pl.pallas_call(functools.partial(tail_kernel, far_size, near_size), out_s...  14.4 us
    pallas_call x1, Pallas kernels, local(): pl.pallas_call(place_kernel, out_shape=(out, out, jax.ShapeDtypeStruct((h...  3.41 us

profile of v6, /device:TPU:0, one launch (start us, length us, event | category | flops | bytes accessed | tf_op | source)
XLA Modules:
  0.0 96.3 jit_solution(11803854266322546578)
XLA Ops:
  0.6 76.7 %exchange.1 = (bf16[16384,128]{1,0:T(8,128)(2,1)S(1)}, bf16[16384,128]{1,0:T(8,128)(2,1)S(1)}, f32[2,128]{1,0:T(2,128)S(1)}) custom-call(bf16[8,2048,128]{2,1,0:T(8,128)(2,1)} %bitcast.10, bf16[8,2048,128]{2,1,0:T(8,128)(2,1)} %bitcast.7, f32[64,8192]{1,0:T(8,128)} %bitcast.11, f32[1,128]{1,0:T(1,128)} %bitcast.12), custom_call_target="tpu_custom_call" | custom-call | tf_op jit(solution)/shard_map/exchange/pallas_call | solution.py:365
  77.3 3.4 %place.1 = (bf16[16384,128]{1,0:T(8,128)(2,1)}, bf16[16384,128]{1,0:T(8,128)(2,1)}, f32[2,128]{1,0:T(2,128)}, f32[2,128]{1,0:T(2,128)S(1)}) custom-call(bf16[16384,128]{1,0:T(8,128)(2,1)S(1)} %get-tuple-element.10.keys_ref, bf16[16384,128]{1,0:T(8,128)(2,1)S(1)} %get-tuple-element.11.values_ref, f32[2,128]{1,0:T(2,128)S(1)} %get-tuple-element.12.scale_ref), custom_call_target="tpu_custom_call" | custom-call | tf_op jit(solution)/shard_map/place/pallas_call | solution.py:401
  80.7 14.4 %tail.1.late_ref = bf16[5376,128]{1,0:T(8,128)(2,1)S(1)} custom-call(bf16[8,2048,128]{2,1,0:T(8,128)(2,1)} %bitcast.8, f32[2,128]{1,0:T(2,128)S(1)} %get-tuple-element.15.after_ref), custom_call_target="tpu_custom_call" | custom-call | tf_op jit(solution)/shard_map/tail/pallas_call | solution.py:413
  95.1 1.1 %place_tail.1 = bf16[16384,128]{1,0:T(8,128)(2,1)} custom-call(bf16[16384,128]{1,0:T(8,128)(2,1)} %get-tuple-element.14.values_ref, bf16[5376,128]{1,0:T(8,128)(2,1)S(1)} %tail.1.late_ref), custom_call_target="tpu_custom_call", output_to_operand_aliasing={{}: (0, {})} | custom-call | tf_op jit(solution)/shard_map/place_tail/pallas_call | solution.py:424
